TPU v7x, 32 devices: a whole 2x2x4 slice. The times are simulated.
32 devices in a mesh: rep: 8 (over y, x, core), tp: 4 (over z).
Axes of the slice: x: 2, y: 2, z: 4, core: 2. Of those that a mesh axis runs over, the one named last changes fastest.
Arguments:
- queries: bfloat16 [2048, 4096], P('rep', 'tp'), may hold values from -120 to 120
- keys_new: bfloat16 [2048, 1024], P('rep', 'tp'), may hold values from -7 to 7
- values_new: bfloat16 [2048, 1024], P('rep', 'tp'), may hold values from -6 to 6
- caches: bfloat16 [16, 2, 4096, 1024], P('rep', None, None, 'tp'), may hold values from -6 to 6
- lengths: int32 [8, 2], replicated, may hold values from 128 to 4096, as said below
- moving: int32 [8], replicated, may hold values from 0 to 1
- destination: int32 [8], replicated, may hold values from 0 to 7, each once
- out_weight: bfloat16 [4096, 4096], P('tp'), may hold values from -0.09375 to 0.09375
Outputs:
- mixed: bfloat16 [2048, 4096], P('rep', 'tp')
- held_cache: bfloat16 [16, 2, 4096, 1024], P('rep', None, None, 'tp')
Inputs may be any that keep to these rules, and one draw needn't show every extreme that they name: `lengths`: multiples of 128; in every draw some slot holds 4096 and some 128. `destination`: each replica receives exactly one failing candidate; it takes the slot that its own failing candidate leaves.
All inputs are finite; a program needn't handle non-finite values.
Results may differ from a plain program's by a relative error of at most 0.014.
Values may be sent and summed in bfloat16 or wider, within the bound.
A program may use at most 64 MiB of HBM per device.

v0:
```python
import jax
import jax.numpy as jnp
from jax import lax
from jax.sharding import PartitionSpec as P

HEAD = 128


masked_score = -1e30
key_block_rows = 512


def attend(query_slot, key_cache, value_cache, length, keys_fresh, values_fresh, block_count):
    span_rows = query_slot.shape[0]
    kv_count = key_cache.shape[1] // HEAD
    group_size = query_slot.shape[1] // (HEAD * kv_count)
    grouped = query_slot.reshape(span_rows, kv_count, group_size, HEAD).transpose(1, 2, 0, 3)
    grouped = grouped.reshape(kv_count, group_size * span_rows, HEAD)
    scale = HEAD ** (-0.5)
    token_of_row = jnp.arange(group_size * span_rows, dtype=jnp.int32) % span_rows

    def absorb(running, key_block, value_block, visible):
        row_max, row_total, weighted = running
        scores = (
            jnp.einsum("gqd,kgd->gqk", grouped, key_block, preferred_element_type=jnp.float32)
            * scale
        )
        scores = jnp.where(visible, scores, masked_score)
        new_max = jnp.maximum(row_max, jnp.max(scores, axis=2))
        rescale = jnp.exp(row_max - new_max)
        weights_block = jnp.where(visible, jnp.exp(scores - new_max[:, :, None]), 0.0)
        row_total = row_total * rescale + jnp.sum(weights_block, axis=2)
        weighted = weighted * rescale[:, :, None] + jnp.einsum(
            "gqk,kgd->gqd",
            weights_block.astype(jnp.bfloat16),
            value_block,
            preferred_element_type=jnp.float32,
        )
        return (new_max, row_total, weighted)

    def cache_step(block_index, running):
        start = block_index * key_block_rows
        key_block = lax.dynamic_slice_in_dim(key_cache, start, key_block_rows, 0).reshape(
            key_block_rows, kv_count, HEAD
        )
        value_block = lax.dynamic_slice_in_dim(value_cache, start, key_block_rows, 0).reshape(
            key_block_rows, kv_count, HEAD
        )
        visible = (start + jnp.arange(key_block_rows, dtype=jnp.int32) < length)[None, None, :]
        return absorb(running, key_block, value_block, visible)

    rows_all = group_size * span_rows
    initial = (
        jnp.full((kv_count, rows_all), masked_score, jnp.float32),
        jnp.zeros((kv_count, rows_all), jnp.float32),
        jnp.zeros((kv_count, rows_all, HEAD), jnp.float32),
    )
    running = lax.fori_loop(0, block_count, cache_step, initial)
    visible = (jnp.arange(span_rows, dtype=jnp.int32)[None, :] <= token_of_row[:, None])[None]
    running = absorb(
        running,
        keys_fresh.reshape(span_rows, kv_count, HEAD),
        values_fresh.reshape(span_rows, kv_count, HEAD),
        visible,
    )
    result = running[2] / running[1][:, :, None]
    result = result.reshape(kv_count, group_size, span_rows, HEAD).transpose(2, 0, 1, 3)
    return result.reshape(span_rows, kv_count * group_size * HEAD).astype(jnp.bfloat16)


def on_device(queries, keys_new, values_new, caches, lengths, moving, destination, out_weight):
    replicas = lax.axis_size("rep")
    own_index = lax.axis_index("rep")
    slot_count = caches.shape[0]
    cache_rows = caches.shape[2]
    width_local = caches.shape[3]
    piece_rows = cache_rows // replicas
    leaving_slot = moving[own_index]
    leaving = lax.dynamic_index_in_dim(caches, leaving_slot, 0, keepdims=False)
    spread = lax.all_to_all(leaving, "rep", split_axis=1, concat_axis=1, tiled=True)
    source_of = jnp.argsort(destination)
    gathered_pieces = spread.reshape(2, replicas, piece_rows, width_local)
    ordered = jnp.take(gathered_pieces, source_of, axis=1).reshape(2, cache_rows, width_local)
    arrived = lax.all_to_all(ordered, "rep", split_axis=1, concat_axis=1, tiled=True)
    anchor = source_of[own_index]
    incoming_length = lengths[anchor, moving[anchor]]
    updated = lax.dynamic_update_index_in_dim(caches, arrived, leaving_slot, 0)
    own_lengths = lengths[own_index]
    held_lengths = jnp.where(jnp.arange(slot_count) == leaving_slot, incoming_length, own_lengths)
    span_rows = queries.shape[0] // slot_count
    results = []
    for slot_number in range(slot_count):
        length = held_lengths[slot_number]
        block_count = cache_rows // key_block_rows
        lower = slot_number * span_rows
        results.append(
            attend(
                queries[lower : lower + span_rows],
                updated[slot_number, 0],
                updated[slot_number, 1],
                length,
                keys_new[lower : lower + span_rows],
                values_new[lower : lower + span_rows],
                block_count,
            )
        )
    attended = jnp.concatenate(results, axis=0)
    partial_value = jnp.dot(attended, out_weight, preferred_element_type=jnp.float32)
    mixed = lax.psum_scatter(
        partial_value.astype(jnp.bfloat16), "tp", scatter_dimension=1, tiled=True
    )
    return (mixed, updated)


def solution(mesh):
    in_specs = (
        P("rep", "tp"),
        P("rep", "tp"),
        P("rep", "tp"),
        P("rep", None, None, "tp"),
        P(),
        P(),
        P(),
        P("tp", None),
    )
    out_specs = (P("rep", "tp"), P("rep", None, None, "tp"))
    return jax.shard_map(
        on_device, mesh=mesh, in_specs=in_specs, out_specs=out_specs, check_vma=False
    )
```

profile of v0, /device:TPU:0, one launch (start us, length us, event | category | flops | bytes accessed | tf_op | source)
XLA Modules:
  0.0 365.8 jit_solution(7094466064213119870)
XLA Ops:
  7.2 7.3 %copy.152 = bf16[2,2,4096,256]{3,2,1,0:T(8,128)(2,1)} copy(bf16[2,2,4096,256]{3,2,1,0:T(8,128)(2,1)} %param.15) | data formatting | bytes 16777216
  20.5 2.5 constant_dynamic-slice_fusion.4
  23.0 27.2 %copy.117 = bf16[1,2,4096,256]{3,1,2,0:T(2,128)(2,1)} copy(bf16[1,2,4096,256]{3,2,1,0:T(8,128)(2,1)S(1)} %constant_dynamic-slice_fusion.4) | data formatting | bytes 8388608 | tf_op jit(solution)/shard_map/jit(dynamic_index_in_dim)/dynamic_slice | solution.py:79
  50.2 5.2 %all-to-all-start = ((bf16[2,4096,256]{2,0,1:T(2,128)(2,1)}), bf16[2,4096,256]{2,0,1:T(2,128)(2,1)}, u32[]{:S(2)}, u32[]{:S(2)}) async-start(bf16[2,4096,256]{2,0,1:T(2,128)(2,1)} %bitcast.118), calls=%async_computation | async-start | bytes 8388608 | tf_op jit(solution)/shard_map/all_to_all | solution.py:80
  55.5 49.1 %all-to-all-done = bf16[2,4096,256]{2,0,1:T(2,128)(2,1)} async-done(((bf16[2,4096,256]{2,0,1:T(2,128)(2,1)}), bf16[2,4096,256]{2,0,1:T(2,128)(2,1)}, u32[]{:S(2)}, u32[]{:S(2)}) %all-to-all-start) | async-done | bytes 4194336 | tf_op jit(solution)/shard_map/all_to_all | solution.py:80
  104.5 4.7 %copy.72 = bf16[2,4096,256]{2,1,0:T(8,128)(2,1)} copy(bf16[2,4096,256]{2,0,1:T(2,128)(2,1)} %all-to-all-done) | data formatting | bytes 8388608 | tf_op jit(solution)/shard_map/all_to_all | solution.py:80
  109.2 4.9 %gather_fusion = bf16[8,2,512,256]{3,2,1,0:T(8,128)(2,1)} fusion(bf16[2,8,512,256]{3,2,1,0:T(8,128)(2,1)} %bitcast.119, s32[1024]{0:T(1024)S(1)} %pad_clamp_fusion), kind=kCustom, calls=%fused_computation | custom fusion | bytes 8388640 | tf_op jit(solution)/shard_map/jit(_take)/gather | solution.py:83
  114.2 2.5 copy.73
  117.7 27.2 %copy.74 = bf16[2,4096,256]{2,0,1:T(2,128)(2,1)} copy(bf16[2,4096,256]{2,1,0:T(8,128)(2,1)S(1)} %bitcast_select_fusion) | data formatting | bytes 8388608 | tf_op jit(solution)/shard_map/jit(_take)/select_n | solution.py:83
  144.9 4.7 %all-to-all-start.1 = ((bf16[2,4096,256]{2,0,1:T(2,128)(2,1)}), bf16[2,4096,256]{2,0,1:T(2,128)(2,1)}, u32[]{:S(2)}, u32[]{:S(2)}) async-start(bf16[2,4096,256]{2,0,1:T(2,128)(2,1)} %copy.74), calls=%async_computation.1 | async-start | bytes 8388608 | tf_op jit(solution)/shard_map/all_to_all | solution.py:84
  154.8 1.2 compare_select_fusion.1
  156.7 1.1 fusion.62
  157.8 1.1 fusion.63
  159.0 39.7 %all-to-all-done.1 = bf16[2,4096,256]{2,0,1:T(2,128)(2,1)} async-done(((bf16[2,4096,256]{2,0,1:T(2,128)(2,1)}), bf16[2,4096,256]{2,0,1:T(2,128)(2,1)}, u32[]{:S(2)}, u32[]{:S(2)}) %all-to-all-start.1) | async-done | bytes 4194336 | tf_op jit(solution)/shard_map/all_to_all | solution.py:84
  198.6 4.7 %copy_dynamic-update-slice_fusion = bf16[2,2,4096,256]{3,2,1,0:T(8,128)(2,1)} fusion(bf16[2,2,4096,256]{3,2,1,0:T(8,128)(2,1)} %copy.152, s32[]{:T(128)S(6)} %select_n.120, bf16[1,2,4096,256]{3,1,2,0:T(2,128)(2,1)} %bitcast.9), kind=kLoop, calls=%fused_computation.53 | loop fusion | bytes 8388612 | tf_op jit(solution)/shard_map/jit(dynamic_update_index_in_dim)/dynamic_update_slice | solution.py:87
  203.4 5.9 %slice_bitcast_fusion.2 = (bf16[4096,256]{1,0:T(8,128)(2,1)}, bf16[4096,256]{1,0:T(8,128)(2,1)}, bf16[4096,256]{1,0:T(8,128)(2,1)}, bf16[4096,256]{1,0:T(8,128)(2,1)}) fusion(bf16[2,2,4096,256]{3,2,1,0:T(8,128)(2,1)} %copy_dynamic-update-slice_fusion), kind=kLoop, calls=%fused_computation.57 | loop fusion | bytes 16777216 | tf_op jit(solution)/shard_map/squeeze | solution.py:100
  209.3 47.3 %while.36 = (s32[]{:T(128)}, f32[2,512]{1,0:T(2,128)S(1)}, f32[2,512]{1,0:T(2,128)S(1)}, f32[2,512,128]{2,1,0:T(8,128)}, s32[]{:T(128)}, /*index=5*/bf16[4096,25...) while((s32[]{:T(128)}, f32[2,512]{1,0:T(2,128)S(1)}, ...), condition=%wide.region_4.5_spmd.clone, body=%wide.region_1.4_spmd.clone.sunk | while | flops 275650560 | bytes 10291387 | solution.py:58
  209.3 1.1 constant_dynamic-slice_fusion.7
  212.5 1.8 convolution_add_fusion.6
  214.3 1.1 constant_dynamic-slice_fusion.7
  217.5 2.8 convolution_add_fusion.6
  223.6 2.8 convolution_add_fusion.6
  226.4 1.1 constant_dynamic-slice_fusion.7
  229.6 2.8 convolution_add_fusion.6
  232.5 1.1 constant_dynamic-slice_fusion.7
  235.7 2.8 convolution_add_fusion.6
  241.7 2.8 convolution_add_fusion.6
  244.6 1.1 constant_dynamic-slice_fusion.7
  247.8 2.8 convolution_add_fusion.6
  250.6 1.1 constant_dynamic-slice_fusion.7
  253.8 2.8 convolution_add_fusion.6
  256.7 47.2 %while.37 = (s32[]{:T(128)}, f32[2,512]{1,0:T(2,128)S(1)}, f32[2,512]{1,0:T(2,128)S(1)}, f32[2,512,128]{2,1,0:T(8,128)}, s32[]{:T(128)}, /*index=5*/bf16[4096,25...) while((s32[]{:T(128)}, f32[2,512]{1,0:T(2,128)S(1)}, ...), condition=%wide.region_10.11_spmd.clone, body=%wide.region_7.10_spmd.clone.sunk | while | flops 275650560 | bytes 10291387 | solution.py:58
  256.7 1.1 constant_dynamic-slice_fusion.8
  259.9 1.8 convolution_add_fusion.7
  261.7 1.1 constant_dynamic-slice_fusion.8
  264.9 2.8 convolution_add_fusion.7
  267.7 1.1 constant_dynamic-slice_fusion.8
  270.9 2.8 convolution_add_fusion.7
  273.8 1.1 constant_dynamic-slice_fusion.8
  277.0 2.8 convolution_add_fusion.7
  283.0 2.8 convolution_add_fusion.7
  289.0 2.8 convolution_add_fusion.7
  295.0 2.8 convolution_add_fusion.7
  301.1 2.8 convolution_add_fusion.7
  304.0 1.3 fusion.39
  305.3 1.7 fusion.34
  308.0 7.1 %convolution_convert_fusion = bf16[256,4096]{1,0:T(8,128)(2,1)} fusion(bf16[1024,4096]{1,0:T(8,128)(2,1)} %param.19, bf16[128,1024]{0,1:T(8,128)(2,1)S(1)} %bitcast.128, bf16[128,1024]{0,1:T(8,128)(2,1)S(1)} %bitcast.127), kind=kOutput, calls=%fused_computation.51 | convolution fusion | flops 2149580800 | bytes 11010048 | tf_op jit(solution)/shard_map/dot_general | solution.py:108
  315.1 43.9 %reduce-scatter.2.cloned.1.call-done = bf16[256,1024]{1,0:T(8,128)(2,1)} async-done(((bf16[256,4096]{1,0:T(8,128)(2,1)}), bf16[256,1024]{1,0:T(8,128)(2,1)}) %reduce-scatter.2.cloned.1.call-update) | async-done | bytes 524304 | tf_op jit(solution)/shard_map/reduce_scatter | solution.py:109
  (192 shorter events, 47.8 us)
Async XLA Ops:
  7.2 10.8 %copy-start.6 = (s32[8]{0:T(128)S(1)}, s32[8]{0:T(128)}, u32[]{:S(2)}) copy-start(s32[8]{0:T(128)} %param.17) | copy-start | bytes 100
  7.2 7.3 %copy-start.7 = (s32[8]{0:T(128)S(1)}, s32[8]{0:T(128)}, u32[]{:S(2)}) copy-start(s32[8]{0:T(128)} %param.18) | copy-start | bytes 100
  50.2 54.4 %all-to-all-start = ((bf16[2,4096,256]{2,0,1:T(2,128)(2,1)}), bf16[2,4096,256]{2,0,1:T(2,128)(2,1)}, u32[]{:S(2)}, u32[]{:S(2)}) async-start(bf16[2,4096,256]{2,0,1:T(2,128)(2,1)} %bitcast.118), calls=%async_computation | async-start | bytes 8388608 | tf_op jit(solution)/shard_map/all_to_all | solution.py:80
  144.9 6.3 %copy-start.5 = (s32[8,2]{0,1:T(2,128)S(1)}, s32[8,2]{0,1:T(2,128)}, u32[]{:S(2)}) copy-start(s32[8,2]{0,1:T(2,128)} %param.16) | copy-start | bytes 196
  144.9 7.7 %copy-start.1 = (bf16[256,1024]{1,0:T(8,128)(2,1)S(1)}, bf16[256,1024]{1,0:T(8,128)(2,1)}, u32[]{:S(2)}) copy-start(bf16[256,1024]{1,0:T(8,128)(2,1)} %param.12) | copy-start | bytes 1572868
  144.9 53.8 %all-to-all-start.1 = ((bf16[2,4096,256]{2,0,1:T(2,128)(2,1)}), bf16[2,4096,256]{2,0,1:T(2,128)(2,1)}, u32[]{:S(2)}, u32[]{:S(2)}) async-start(bf16[2,4096,256]{2,0,1:T(2,128)(2,1)} %copy.74), calls=%async_computation.1 | async-start | bytes 8388608 | tf_op jit(solution)/shard_map/all_to_all | solution.py:84
  149.5 3.3 copy-start.2
  149.6 3.8 %copy-start.3 = (bf16[256,256]{1,0:T(8,128)(2,1)S(1)}, bf16[256,256]{1,0:T(8,128)(2,1)}, u32[]{:S(2)}) copy-start(bf16[256,256]{1,0:T(8,128)(2,1)} %param.14) | copy-start | bytes 393220
  149.6 209.4 %reduce-scatter.2.cloned.1.call-start = ((), (), s32[]{:S(2)}) async-start(), calls=%async_computation.3 | async-start | bytes 2621440 | tf_op jit(solution)/shard_map/reduce_scatter | solution.py:109
  256.7 47.3 %copy-start = (f32[2,512,128]{1,2,0:T(8,128)S(1)}, f32[2,512,128]{1,2,0:T(8,128)}, u32[]{:S(2)}) copy-start(f32[2,512,128]{1,2,0:T(8,128)} %get-tuple-element.461) | copy-start | bytes 1572868
  303.9 3.3 copy-start.4
  303.9 3.3 copy-start.8
Sparse Core Ops, SparseCore 0:
  315.2 43.7 reduce-scatter.1
where the time goes:
time: 368 us; the launch traced here: 366 us
  waiting for transfers between devices  133 us (36%)
  local copies, waits for them, and re-layouts  114 us (31%)
  matrix products  63.8 us (17%)
  other arithmetic  24.7 us (7%)
  between operations  20.1 us (5%)
  starting transfers between devices  10.1 us (3%)
    all_to_all x1, waiting for transfers between devices, on_device(): lax.all_to_all(leaving, 'rep', split_axis=1, concat_axis=1, tiled=True)  49.1 us
    dot_general x18, matrix products, absorb(): jnp.einsum('gqk,kgd->gqd', weights_block.astype(jnp.bfloat16), value_bloc...  45.6 us
    reduce_scatter x1, waiting for transfers between devices, on_device(): lax.psum_scatter(partial_value.astype(jnp.bfloat16), 'tp', scatter_dimens...  43.9 us
    all_to_all x1, waiting for transfers between devices, on_device(): lax.all_to_all(ordered, 'rep', split_axis=1, concat_axis=1, tiled=True)  39.7 us
    dynamic_slice x2, local copies, waits for them, and re-layouts, on_device(): leaving = lax.dynamic_index_in_dim(caches, leaving_slot, 0, keepdims=False)  29.7 us
    select_n x1, local copies, waits for them, and re-layouts, on_device(): jnp.take(gathered_pieces, source_of, axis=1)  27.2 us
    dynamic_slice x32, local copies, waits for them, and re-layouts, cache_step(): lax.dynamic_slice_in_dim(value_cache, start, key_block_rows, 0)  19.3 us
    dot_general x18, matrix products, absorb(): jnp.einsum('gqd,kgd->gqk', grouped, key_block, preferred_element_type=jnp...  11.1 us
  transfers between devices with their start and end apart: 3, of which 3 were waited for; matrix products, arithmetic and copies ran while one was open for 2% of the time, Pallas kernels for 0%

commit v1 on v0

v1 whole, which is shorter than its diff:
```python
import functools

import jax
import jax.numpy as jnp
from jax import lax
from jax.experimental import pallas as pl
from jax.experimental.pallas import tpu as pltpu
from jax.sharding import PartitionSpec as P

HEAD = 128
BLOCK = 512
LOG2E = 1.4426950408889634
masked_score = -1e30


def slot_kernel(
    scalars, source, query_t, keys_fresh, values_fresh, *rest, aliased, kv_count, group
):
    if aliased:
        rest = rest[1:]
    held, attended, cache, row_max, row_total, weighted, in_sem, out_sem = rest
    taken, target, length = scalars[0], scalars[1], scalars[2]
    rows = cache.shape[1]
    blocks = rows // BLOCK
    span = keys_fresh.shape[0]
    factor = HEAD ** (-0.5) * LOG2E

    def fetch(block, part):
        at = pl.ds(pl.multiple_of(block * BLOCK, BLOCK), BLOCK)
        return pltpu.make_async_copy(
            source.at[taken, part, at], cache.at[part, at], in_sem.at[block, part]
        )

    def put(block, part):
        at = pl.ds(pl.multiple_of(block * BLOCK, BLOCK), BLOCK)
        return pltpu.make_async_copy(
            cache.at[part, at], held.at[target, part, at], out_sem.at[block, part]
        )

    for block in range(blocks):
        for part in range(2):
            fetch(block, part).start()

    def scores_of(head, keys):
        return lax.dot_general(
            keys,
            query_t[head],
            (((1,), (0,)), ((), ())),
            preferred_element_type=jnp.float32,
        )

    def mix(values, weights):
        return lax.dot_general(
            values,
            weights.astype(jnp.bfloat16),
            (((0,), (0,)), ((), ())),
            preferred_element_type=jnp.float32,
        )

    key_at = lax.broadcasted_iota(jnp.int32, (span, group * span), 0)
    token_at = lax.broadcasted_iota(jnp.int32, (span, group * span), 1) % span
    for head in range(kv_count):
        lanes = slice(head * HEAD, (head + 1) * HEAD)
        scores = jnp.where(
            key_at <= token_at, scores_of(head, keys_fresh[:, lanes]), masked_score
        )
        new_max = jnp.max(scores, axis=0, keepdims=True)
        weights = jnp.exp2((scores - new_max) * factor)
        row_max[head] = new_max
        row_total[head] = jnp.sum(weights, axis=0, keepdims=True)
        weighted[head] = mix(values_fresh[:, lanes], weights)

    def absorb(block, masked):
        start = pl.multiple_of(block * BLOCK, BLOCK)
        at = pl.ds(start, BLOCK)
        for head in range(kv_count):
            lanes = slice(head * HEAD, (head + 1) * HEAD)
            scores = scores_of(head, cache[0, at, lanes])
            if masked:
                position = start + lax.broadcasted_iota(jnp.int32, scores.shape, 0)
                scores = jnp.where(position < length, scores, masked_score)
            old_max = row_max[head]
            new_max = jnp.maximum(old_max, jnp.max(scores, axis=0, keepdims=True))
            rescale = jnp.exp2((old_max - new_max) * factor)
            weights = jnp.exp2((scores - new_max) * factor)
            row_max[head] = new_max
            row_total[head] = row_total[head] * rescale + jnp.sum(
                weights, axis=0, keepdims=True
            )
            weighted[head] = weighted[head] * rescale + mix(cache[1, at, lanes], weights)

    def step(block, carry):
        for part in range(2):
            fetch(block, part).wait()
            put(block, part).start()
        start = block * BLOCK

        @pl.when(start + BLOCK <= length)
        def _():
            absorb(block, False)

        @pl.when((start < length) & (length < start + BLOCK))
        def _():
            absorb(block, True)

        return carry

    lax.fori_loop(0, blocks, step, 0)
    for head in range(kv_count):
        result = (weighted[head] / row_total[head]).T
        for member in range(group):
            lanes = slice((head * group + member) * HEAD, (head * group + member + 1) * HEAD)
            attended[:, lanes] = result[member * span : (member + 1) * span].astype(
                jnp.bfloat16
            )
    for block in range(blocks):
        for part in range(2):
            put(block, part).wait()


def attend_slot(scalars, source, query_t, keys_fresh, values_fresh, held, held_shape):
    kv_count, _, columns = query_t.shape
    span = keys_fresh.shape[0]
    group = columns // span
    rows, width = source.shape[2:]
    aliased = held is not None
    anywhere = pl.BlockSpec(memory_space=pl.ANY)
    vmem = pl.BlockSpec(memory_space=pltpu.VMEM)
    operands = [scalars, source, query_t, keys_fresh, values_fresh]
    in_specs = [pl.BlockSpec(memory_space=pltpu.SMEM), anywhere, vmem, vmem, vmem]
    if aliased:
        operands.append(held)
        in_specs.append(anywhere)
    blocks = rows // BLOCK
    return pl.pallas_call(
        functools.partial(slot_kernel, aliased=aliased, kv_count=kv_count, group=group),
        out_shape=(
            jax.ShapeDtypeStruct(held_shape, jnp.bfloat16),
            jax.ShapeDtypeStruct((span, kv_count * group * HEAD), jnp.bfloat16),
        ),
        in_specs=in_specs,
        out_specs=(anywhere, vmem),
        scratch_shapes=[
            pltpu.VMEM((2, rows, width), jnp.bfloat16),
            pltpu.VMEM((kv_count, 1, columns), jnp.float32),
            pltpu.VMEM((kv_count, 1, columns), jnp.float32),
            pltpu.VMEM((kv_count, HEAD, columns), jnp.float32),
            pltpu.SemaphoreType.DMA((blocks, 2)),
            pltpu.SemaphoreType.DMA((blocks, 2)),
        ],
        input_output_aliases={5: 0} if aliased else {},
        compiler_params=pltpu.CompilerParams(vmem_limit_bytes=40 * 1024 * 1024),
        cost_estimate=pl.CostEstimate(
            flops=4 * kv_count * columns * (rows + span) * HEAD,
            bytes_accessed=8 * rows * width,
            transcendentals=kv_count * columns * (rows + span),
        ),
    )(*operands)


def on_device(queries, keys_new, values_new, caches, lengths, moving, destination, out_weight):
    replicas = lax.axis_size("rep")
    own_index = lax.axis_index("rep")
    slot_count, _, cache_rows, width = caches.shape
    span = queries.shape[0] // slot_count
    kv_count = width // HEAD
    group = queries.shape[1] // width
    leaving_slot = moving[own_index]
    staying_slot = 1 - leaving_slot
    leaving = lax.dynamic_index_in_dim(caches, leaving_slot, 0, keepdims=False)
    piece_rows = 2 * cache_rows // replicas
    pieces = leaving.reshape(replicas, piece_rows, width)
    spread = lax.all_to_all(pieces, "rep", split_axis=0, concat_axis=0, tiled=True)
    source_of = jnp.argsort(destination)
    ordered = jnp.take(spread, source_of, axis=0, mode="clip")
    arrived = lax.all_to_all(ordered, "rep", split_axis=0, concat_axis=0, tiled=True)
    arrived = arrived.reshape(1, 2, cache_rows, width)

    anchor = source_of[own_index]
    incoming_length = lengths[anchor, moving[anchor]]
    staying_length = lengths[own_index, staying_slot]
    query_t = (
        queries.reshape(slot_count, span, kv_count, group, HEAD)
        .transpose(0, 2, 4, 3, 1)
        .reshape(slot_count, kv_count, HEAD, group * span)
    )
    keys_by_slot = keys_new.reshape(slot_count, span, width)
    values_by_slot = values_new.reshape(slot_count, span, width)

    def pick(array, slot):
        return lax.dynamic_index_in_dim(array, slot, 0, keepdims=False)

    def project(attended):
        partial_value = jnp.dot(attended, out_weight, preferred_element_type=jnp.float32)
        return lax.psum_scatter(
            partial_value.astype(jnp.bfloat16), "tp", scatter_dimension=1, tiled=True
        )

    held, staying_attended = attend_slot(
        jnp.stack([staying_slot, staying_slot, staying_length]),
        caches,
        pick(query_t, staying_slot),
        pick(keys_by_slot, staying_slot),
        pick(values_by_slot, staying_slot),
        None,
        caches.shape,
    )
    staying_mixed = project(staying_attended)
    held, arrived_attended = attend_slot(
        jnp.stack([jnp.zeros_like(leaving_slot), leaving_slot, incoming_length]),
        arrived,
        pick(query_t, leaving_slot),
        pick(keys_by_slot, leaving_slot),
        pick(values_by_slot, leaving_slot),
        held,
        caches.shape,
    )
    arrived_mixed = project(arrived_attended)
    mixed = jnp.where(
        leaving_slot == 0,
        jnp.concatenate([arrived_mixed, staying_mixed], axis=0),
        jnp.concatenate([staying_mixed, arrived_mixed], axis=0),
    )
    return (mixed, held)


def solution(mesh):
    in_specs = (
        P("rep", "tp"),
        P("rep", "tp"),
        P("rep", "tp"),
        P("rep", None, None, "tp"),
        P(),
        P(),
        P(),
        P("tp", None),
    )
    out_specs = (P("rep", "tp"), P("rep", None, None, "tp"))
    return jax.shard_map(
        on_device, mesh=mesh, in_specs=in_specs, out_specs=out_specs, check_vma=False
    )
```

time: 368 us -> 187 us (0.51)
  local copies, waits for them, and re-layouts: 114 us -> 16.5 us
  matrix products: 63.8 us -> 11.3 us
  waiting for transfers between devices: 133 us -> 105 us
  other arithmetic: 24.7 us -> 5.84 us
  Pallas kernels: 0 us -> 16.1 us
    dot_general x37 -> x2, matrix products: 63.8 us -> 11.3 us  [project(): jnp.dot(attended, out_weight, preferred_element_type=jnp.float32)]
    select_n x1 -> x0, local copies, waits for them, and re-layouts: 27.2 us -> none  [on_device(): jnp.take(gathered_pieces, source_of, axis=1)]
    dynamic_slice x2 -> x1, local copies, waits for them, and re-layouts: 29.7 us -> 4.47 us  [on_device(): leaving = lax.dynamic_index_in_dim(caches, leaving_slot, 0, keepdims=False)]
    dynamic_slice x50 -> x0, local copies, waits for them, and re-layouts: 22.4 us -> none  [the longest x32 19.3 us: cache_step(): lax.dynamic_slice_in_dim(value_cache, start, key_block_rows, 0)]
    pallas_call x0 -> x2, Pallas kernels: none -> 16.1 us  [attend_slot(): pl.pallas_call(functools.partial(slot_kernel, aliased=aliased, kv_count=k...]
    reduce_scatter x1 -> x2, waiting for transfers between devices: 43.9 us -> 29.5 us  [project(): lax.psum_scatter(partial_value.astype(jnp.bfloat16), 'tp', scatter_dimens...]
    all_to_all x2, waiting for transfers between devices: 88.7 us -> 75.2 us  [the longest x1 49.1 us: on_device(): lax.all_to_all(pieces, 'rep', split_axis=0, concat_axis=0, tiled=True)]
    reduce_sum x17 -> x0, other arithmetic: 10.8 us -> none  [absorb(): row_total = row_total * rescale + jnp.sum(weights_block, axis=2)]
  transfers between devices with their start and end apart: 3 -> 4, of which waited for: 3 -> 3; matrix products, arithmetic and copies ran while one was open for 2% -> 8% of each run, Pallas kernels for 0% -> 9%
where the time goes in v1:
time: 187 us; the launch traced here: 186 us
  waiting for transfers between devices  105 us (56%)
  between operations  21.5 us (11%)
  local copies, waits for them, and re-layouts  16.5 us (9%)
  Pallas kernels  16.1 us (9%)
  matrix products  11.3 us (6%)
  starting transfers between devices  9.84 us (5%)
  other arithmetic  5.84 us (3%)
    all_to_all x1, waiting for transfers between devices, on_device(): lax.all_to_all(pieces, 'rep', split_axis=0, concat_axis=0, tiled=True)  49.1 us
    reduce_scatter x2, waiting for transfers between devices, project(): lax.psum_scatter(partial_value.astype(jnp.bfloat16), 'tp', scatter_dimens...  29.5 us
    all_to_all x1, waiting for transfers between devices, on_device(): lax.all_to_all(ordered, 'rep', split_axis=0, concat_axis=0, tiled=True)  26 us
    pallas_call x2, Pallas kernels, attend_slot(): pl.pallas_call(functools.partial(slot_kernel, aliased=aliased, kv_count=k...  16.1 us
    dot_general x2, matrix products, project(): jnp.dot(attended, out_weight, preferred_element_type=jnp.float32)  11.3 us
    all_to_all x1, starting transfers between devices, on_device(): lax.all_to_all(pieces, 'rep', split_axis=0, concat_axis=0, tiled=True)  5.2 us
    gather x1, local copies, waits for them, and re-layouts, on_device(): ordered = jnp.take(spread, source_of, axis=0, mode='clip')  4.94 us
    all_to_all x1, starting transfers between devices, on_device(): lax.all_to_all(ordered, 'rep', split_axis=0, concat_axis=0, tiled=True)  4.56 us
  transfers between devices with their start and end apart: 4, of which 3 were waited for; matrix products, arithmetic and copies ran while one was open for 8% of the time, Pallas kernels for 9%

profile of v1, /device:TPU:0, one launch (start us, length us, event | category | flops | bytes accessed | tf_op | source)
XLA Modules:
  0.0 185.9 jit_solution(3261184730710997163)
XLA Ops:
  7.2 1.6 sort.17
  8.8 0.6 dynamic_slice.40
  11.3 1.3 fusion.1
  14.4 4.5 %constant_dynamic-slice_fusion = bf16[1,2,4096,256]{3,2,1,0:T(8,128)(2,1)} fusion(bf16[2,2,4096,256]{3,2,1,0:T(8,128)(2,1)} %source.1, s32[]{:T(128)S(6)} %select_n.39), kind=kLoop, calls=%fused_computation.11 | loop fusion | bytes 8388612 | tf_op jit(solution)/shard_map/jit(dynamic_index_in_dim)/dynamic_slice | solution.py:170
  18.9 5.2 %all-to-all-start = ((bf16[8,1024,256]{2,1,0:T(8,128)(2,1)}), bf16[8,1024,256]{2,1,0:T(8,128)(2,1)}, u32[]{:S(2)}, u32[]{:S(2)}) async-start(bf16[8,1024,256]{2,1,0:T(8,128)(2,1)} %bitcast.27), calls=%async_computation | async-start | bytes 8388608 | tf_op jit(solution)/shard_map/all_to_all | solution.py:173
  24.1 0.0 copy-start.1
  24.1 0.0 copy-start.4
  24.1 0.0 copy-start.2
  24.1 0.0 copy-start.3
  24.1 49.1 %all-to-all-done = bf16[8,1024,256]{2,1,0:T(8,128)(2,1)} async-done(((bf16[8,1024,256]{2,1,0:T(8,128)(2,1)}), bf16[8,1024,256]{2,1,0:T(8,128)(2,1)}, u32[]{:S(2)}, u32[]{:S(2)}) %all-to-all-start) | async-done | bytes 4194336 | tf_op jit(solution)/shard_map/all_to_all | solution.py:173
  73.3 4.9 %gather_fusion = bf16[8,1024,256]{2,1,0:T(8,128)(2,1)} fusion(bf16[8,1024,256]{2,1,0:T(8,128)(2,1)} %all-to-all-done, s32[1024]{0:T(1024)S(1)} %pad_clamp_fusion), kind=kCustom, calls=%fused_computation | custom fusion | bytes 8388640 | tf_op jit(solution)/shard_map/jit(_take)/gather | solution.py:175
  78.2 4.6 %all-to-all-start.1 = ((bf16[8,1024,256]{2,1,0:T(8,128)(2,1)}), bf16[8,1024,256]{2,1,0:T(8,128)(2,1)}, u32[]{:S(2)}, u32[]{:S(2)}) async-start(bf16[8,1024,256]{2,1,0:T(8,128)(2,1)} %gather_fusion), calls=%async_computation.1 | async-start | bytes 8388608 | tf_op jit(solution)/shard_map/all_to_all | solution.py:176
  82.8 0.0 reduce-scatter.5.cloned.1.call-start
  85.3 0.0 copy-done.1
  85.3 0.4 reshape.25
  85.6 0.5 copy.11
  86.2 0.2 reshape.26
  87.0 0.0 copy-done.4
  87.0 0.7 fusion
  87.7 0.7 pad_add_fusion.1.scalars
  88.4 0.0 copy-done.2
  88.5 0.0 copy-done.3
  88.5 0.0 copy-start
  88.5 3.4 %copy-done = bf16[2,2,4096,256]{3,2,1,0:T(8,128)(2,1)S(1)} copy-done((bf16[2,2,4096,256]{3,2,1,0:T(8,128)(2,1)S(1)}, bf16[2,2,4096,256]{3,2,1,0:T(8,128)(2,1)}, u32[]{:S(2)}) %copy-start) | copy-done | bytes 8388632
  91.9 6.8 %shard_map.95 = (bf16[2,2,4096,256]{3,2,1,0:T(8,128)(2,1)}, bf16[128,1024]{1,0:T(8,128)(2,1)S(1)}) custom-call(s32[3]{0:T(128)S(1)} %pad_add_fusion.1.scalars, bf16[2,2,4096,256]{3,2,1,0:T(8,128)(2,1)S(1)} %copy-done, bf16[2,128,512]{2,1,0:T(8,128)(2,1)S(1)} %get-tuple-element.13.query_t, bf16[128,256]{1,0:T(8,128)(2,1)S(1)} %get-tuple-element.22.keys_fresh, ...), custom_call_target="tpu_custom_call" | custom-call | flops 2214592512 | bytes 8388608 | tf_op jit(solution)/shard_map/pallas_call | solution.py:135
  98.7 5.7 %convolution_convert_fusion = bf16[128,4096]{1,0:T(8,128)(2,1)} fusion(bf16[128,1024]{1,0:T(8,128)(2,1)S(1)} %get-tuple-element.10, bf16[1024,4096]{1,0:T(8,128)(2,1)} %param.15), kind=kOutput, calls=%fused_computation.1 | convolution fusion | flops 1074266112 | bytes 9699328 | tf_op jit(solution)/shard_map/dot_general | solution.py:194
  104.4 0.0 reduce-scatter.5.cloned.1.call-update
  104.5 0.0 reduce-scatter.3.cloned.1.call-start
  104.5 1.3 pad_add_fusion.scalars
  105.8 26.0 %all-to-all-done.1 = bf16[8,1024,256]{2,1,0:T(8,128)(2,1)} async-done(((bf16[8,1024,256]{2,1,0:T(8,128)(2,1)}), bf16[8,1024,256]{2,1,0:T(8,128)(2,1)}, u32[]{:S(2)}, u32[]{:S(2)}) %all-to-all-start.1) | async-done | bytes 4194336 | tf_op jit(solution)/shard_map/all_to_all | solution.py:176
  131.9 9.3 %shard_map.96 = (bf16[2,2,4096,256]{3,2,1,0:T(8,128)(2,1)}, bf16[128,1024]{1,0:T(8,128)(2,1)S(1)}) custom-call(s32[3]{0:T(128)S(1)} %pad_add_fusion.scalars, bf16[1,2,4096,256]{3,2,1,0:T(8,128)(2,1)} %bitcast.5.source, bf16[2,128,512]{2,1,0:T(8,128)(2,1)S(1)} %get-tuple-element.12.query_t, ...), custom_call_target="tpu_custom_call", output_to_operand_aliasing={{0}: (5, {})} | custom-call | flops 2214592512 | bytes 8388608 | tf_op jit(solution)/shard_map/pallas_call | solution.py:135
  141.2 5.6 %convolution_convert_fusion.1 = bf16[128,4096]{1,0:T(8,128)(2,1)} fusion(bf16[128,1024]{1,0:T(8,128)(2,1)S(1)} %get-tuple-element.9, bf16[1024,4096]{1,0:T(8,128)(2,1)} %param.15), kind=kOutput, calls=%fused_computation.2 | convolution fusion | flops 1074266112 | bytes 9699328 | tf_op jit(solution)/shard_map/dot_general | solution.py:194
  146.8 0.0 reduce-scatter.3.cloned.1.call-update
  147.4 0.0 reduce-scatter.5.cloned.1.call-done
  147.4 29.4 %reduce-scatter.3.cloned.1.call-done = bf16[128,1024]{1,0:T(8,128)(2,1)} async-done(((bf16[128,4096]{1,0:T(8,128)(2,1)}), bf16[128,1024]{1,0:T(8,128)(2,1)}) %reduce-scatter.3.cloned.1.call-update) | async-done | bytes 262160 | tf_op jit(solution)/shard_map/reduce_scatter | solution.py:195
  176.9 2.2 %maximum_select_fusion = bf16[256,1024]{1,0:T(8,128)(2,1)} fusion(bf16[128,1024]{1,0:T(8,128)(2,1)} %reduce-scatter.5.cloned.1.call-done, bf16[128,1024]{1,0:T(8,128)(2,1)} %reduce-scatter.3.cloned.1.call-done, pred[]{:T(512)S(6)} %eq.3), kind=kLoop, calls=%fused_computation.3 | loop fusion | flops 2359296 | bytes 1048577 | tf_op jit(solution)/shard_map/jit(_where)/select_n | solution.py:219
  (4 shorter events, 0.1 us)
Async XLA Ops:
  18.9 54.4 %all-to-all-start = ((bf16[8,1024,256]{2,1,0:T(8,128)(2,1)}), bf16[8,1024,256]{2,1,0:T(8,128)(2,1)}, u32[]{:S(2)}, u32[]{:S(2)}) async-start(bf16[8,1024,256]{2,1,0:T(8,128)(2,1)} %bitcast.27), calls=%async_computation | async-start | bytes 8388608 | tf_op jit(solution)/shard_map/all_to_all | solution.py:173
  24.1 61.2 %copy-start.1 = (bf16[256,1024]{1,0:T(8,128)(2,1)S(1)}, bf16[256,1024]{1,0:T(8,128)(2,1)}, u32[]{:S(2)}) copy-start(bf16[256,1024]{1,0:T(8,128)(2,1)} %param.8) | copy-start | bytes 1572868
  24.1 63.0 %copy-start.4 = (s32[8,2]{0,1:T(2,128)S(1)}, s32[8,2]{0,1:T(2,128)}, u32[]{:S(2)}) copy-start(s32[8,2]{0,1:T(2,128)} %param.12) | copy-start | bytes 196
  24.1 64.4 %copy-start.2 = (bf16[256,256]{1,0:T(8,128)(2,1)S(1)}, bf16[256,256]{1,0:T(8,128)(2,1)}, u32[]{:S(2)}) copy-start(bf16[256,256]{1,0:T(8,128)(2,1)} %param.10) | copy-start | bytes 393220
  24.1 64.4 %copy-start.3 = (bf16[256,256]{1,0:T(8,128)(2,1)S(1)}, bf16[256,256]{1,0:T(8,128)(2,1)}, u32[]{:S(2)}) copy-start(bf16[256,256]{1,0:T(8,128)(2,1)} %param.9) | copy-start | bytes 393220
  78.2 53.7 %all-to-all-start.1 = ((bf16[8,1024,256]{2,1,0:T(8,128)(2,1)}), bf16[8,1024,256]{2,1,0:T(8,128)(2,1)}, u32[]{:S(2)}, u32[]{:S(2)}) async-start(bf16[8,1024,256]{2,1,0:T(8,128)(2,1)} %gather_fusion), calls=%async_computation.1 | async-start | bytes 8388608 | tf_op jit(solution)/shard_map/all_to_all | solution.py:176
  82.8 64.7 %reduce-scatter.5.cloned.1.call-start = ((), (), s32[]{:S(2)}) async-start(), calls=%async_computation.5 | async-start | bytes 1310720 | tf_op jit(solution)/shard_map/reduce_scatter | solution.py:195
  88.5 3.4 %copy-start = (bf16[2,2,4096,256]{3,2,1,0:T(8,128)(2,1)S(1)}, bf16[2,2,4096,256]{3,2,1,0:T(8,128)(2,1)}, u32[]{:S(2)}) copy-start(bf16[2,2,4096,256]{3,2,1,0:T(8,128)(2,1)} %source.1) | copy-start | bytes 25165828
  104.5 72.4 %reduce-scatter.3.cloned.1.call-start = ((), (), s32[]{:S(2)}) async-start(), calls=%async_computation.4 | async-start | bytes 1310720 | tf_op jit(solution)/shard_map/reduce_scatter | solution.py:195
Sparse Core Ops, SparseCore 0:
  104.6 34.0 reduce-scatter.4
  146.9 29.8 reduce-scatter.2
